TPU v7x, 32 devices: a whole 2x2x4 slice. The times are simulated.
32 devices in a mesh: group: 2 (over x), lat: 16 (over z, y, core).
Axes of the slice: x: 2, y: 2, z: 4, core: 2. Of those that a mesh axis runs over, the one named last changes fastest.
Arguments:
- grid_values: bfloat16 [224, 1440, 256], P(('group', 'lat')), parts along dimension 0, may hold values from -630 to 630
- lat_counts: int32 [16], replicated, may hold values from 1 to 7, 96 in all
- owner_wavenumber: int32 [384], replicated, may hold values from 0 to 383, each once
- legendre: bfloat16 [384, 96, 384], P('lat'), may hold values from -0.625 to 0.625
- quad_weight: float32 [96], replicated, may hold values from 0.3 to 3
- spectral_gain: float32 [384, 256], replicated, may hold values from 0.3 to 3
- channel_mix: bfloat16 [256, 256], replicated, may hold values from -0.375 to 0.375
Outputs:
- grid_output: bfloat16 [224, 1440, 256], P(('group', 'lat')), parts along dimension 0
There are 2 independent parts, one for each index of `group`. A program takes and returns all parts, laid end to end along the dimension named above; an argument that names none is the same for every part. Nothing has to cross between parts.
Inputs may be any that keep to these rules, and one draw needn't show every extreme that they name: `lat_counts`: some device has all 7 slots live. `owner_wavenumber`: each wavenumber appears once; device i of lat owns wavenumber slots i * 24 to (i + 1) * 24 - 1.
All inputs are finite; a program needn't handle non-finite values.
Results may differ from a plain program's by a relative error of at most 0.0095.
Values may be sent and summed in bfloat16 or wider, within the bound.
No kernel may reach another device: no remote copies, remote signals or barrier semaphores. Data moves between devices by JAX's collectives and lax.ppermute only.
A program may use at most 64 MiB of HBM per device.

v0:
```python
import math
import jax
import jax.numpy as jnp
from jax import lax
from jax.sharding import PartitionSpec as P


def live_slots(lat_counts, slot_count, live_total):
    devices = lat_counts.shape[0]
    starts = jnp.cumsum(lat_counts) - lat_counts
    device_ids = jnp.arange(devices, dtype=jnp.int32)
    slot_ids = jnp.arange(devices * slot_count, dtype=jnp.int32)
    holder = slot_ids // slot_count
    within = slot_ids - holder * slot_count
    holder_hot = holder[:, None] == device_ids[None, :]
    holder_count = jnp.sum(jnp.where(holder_hot, lat_counts[None, :], 0), axis=1)
    holder_start = jnp.sum(jnp.where(holder_hot, starts[None, :], 0), axis=1)
    slot_valid = within < holder_count
    slot_live = jnp.where(slot_valid, holder_start + within, 0)
    live_ids = jnp.arange(live_total, dtype=jnp.int32)
    reached = (starts[None, :] <= live_ids[:, None]).astype(jnp.int32)
    source = jnp.sum(reached, axis=1) - 1
    source_hot = source[:, None] == device_ids[None, :]
    source_start = jnp.sum(jnp.where(source_hot, starts[None, :], 0), axis=1)
    live_slot = source * slot_count + live_ids - source_start
    return (slot_valid, slot_live, live_slot)


def wave_angles(wave_list, longitudes):
    points = jnp.arange(longitudes, dtype=jnp.int32)
    phase = wave_list[:, None] * points[None, :] % longitudes
    return phase.astype(jnp.float32) * (2.0 * math.pi / longitudes)


def forward_table(wave_list, longitudes):
    angle = wave_angles(wave_list, longitudes)
    factor = 1.0 / math.sqrt(longitudes)
    return jnp.stack([jnp.cos(angle) * factor, -jnp.sin(angle) * factor], axis=1).astype(
        jnp.bfloat16
    )


def inverse_table(wave_list, longitudes):
    angle = wave_angles(wave_list, longitudes)
    factor = 1.0 / math.sqrt(longitudes)
    doubled = jnp.where(wave_list > 0, 2.0, 1.0).astype(jnp.float32)[:, None] * factor
    return jnp.stack([jnp.cos(angle) * doubled, -jnp.sin(angle) * doubled], axis=1).astype(
        jnp.bfloat16
    )


def body(
    grid_values, lat_counts, owner_wavenumber, legendre, quad_weight, spectral_gain, channel_mix
):
    slot_count, longitudes, channels = grid_values.shape
    my_index = lax.axis_index("lat")
    wave_count = owner_wavenumber.shape[0]
    wave_share, live_total, degrees = legendre.shape
    slot_valid, slot_live, live_slot = live_slots(lat_counts, slot_count, live_total)
    local_valid = lax.dynamic_slice_in_dim(slot_valid, my_index * slot_count, slot_count)
    row_weight = local_valid.astype(jnp.float32)[:, None, None]
    widened = grid_values.astype(jnp.float32) * row_weight
    totals = lax.psum(
        (jnp.sum(widened, axis=(0, 1)), jnp.sum(widened * widened, axis=(0, 1))), "lat"
    )
    points = live_total * longitudes
    channel_mean = totals[0] / points
    variance = totals[1] / points - channel_mean * channel_mean
    normed = (
        (grid_values.astype(jnp.float32) - channel_mean) * lax.rsqrt(variance + 1e-05) * row_weight
    ).astype(jnp.bfloat16)
    forward_flat = forward_table(owner_wavenumber, longitudes).reshape(2 * wave_count, longitudes)
    spectra = jnp.einsum("skc,qk->sqc", normed, forward_flat, preferred_element_type=jnp.float32)
    spectra = spectra.astype(jnp.bfloat16).reshape(slot_count, wave_count, 2, normed.shape[2])
    received = lax.all_to_all(spectra, "lat", split_axis=1, concat_axis=0, tiled=True)
    own_waves = lax.dynamic_slice_in_dim(owner_wavenumber, my_index * wave_share, wave_share)
    degree_mask = (jnp.arange(degrees, dtype=jnp.int32)[None, :] >= own_waves[:, None]).astype(
        jnp.float32
    )
    gathered = jnp.take(received, live_slot, axis=0)
    weighted = (gathered.astype(jnp.float32) * quad_weight[:, None, None, None]).astype(
        jnp.bfloat16
    )
    coefficient = jnp.einsum(
        "rgl,grtc->rltc", legendre, weighted, preferred_element_type=jnp.float32
    )
    filtered = (
        coefficient * degree_mask[:, :, None, None] * spectral_gain[None, :, None, :]
    ).astype(jnp.bfloat16)
    mixed = jnp.dot(filtered.reshape(-1, channels), channel_mix, preferred_element_type=jnp.float32)
    mixed = mixed.astype(jnp.bfloat16).reshape(wave_share, degrees, 2, channels)
    synthesis = jnp.einsum(
        "rgl,rltc->grtc", legendre, mixed, preferred_element_type=jnp.float32
    ).astype(jnp.bfloat16)
    outgoing = jnp.where(
        slot_valid[:, None, None, None],
        jnp.take(synthesis, slot_live, axis=0),
        jnp.zeros((), jnp.bfloat16),
    )
    inverse_flat = inverse_table(owner_wavenumber, longitudes).reshape(2 * wave_count, longitudes)
    returned = lax.all_to_all(outgoing, "lat", split_axis=0, concat_axis=1, tiled=True)
    flat_back = returned.reshape(slot_count, 2 * wave_count, returned.shape[3])
    return jnp.einsum(
        "sqc,qk->skc", flat_back, inverse_flat, preferred_element_type=jnp.float32
    ).astype(jnp.bfloat16)


def solution(mesh):
    return jax.shard_map(
        body,
        mesh=mesh,
        in_specs=(P(("group", "lat"), None, None), P(), P(), P("lat", None, None), P(), P(), P()),
        out_specs=P(("group", "lat"), None, None),
        check_vma=False,
    )
```

profile of v0, /device:TPU:15, one launch (start us, length us, event | category | flops | bytes accessed | tf_op | source)
XLA Modules:
  0.0 337.3 jit_solution(7146616504685830470)
XLA Ops:
  0.0 0.0 copy-start
  0.0 0.9 copy.57
  0.9 0.1 reduce
  1.0 0.7 sub.72
  1.7 0.7 select_multiply_fusion
  2.4 10.7 %multiply_convert_fusion.4 = (bf16[384,1,1440]{0,2,1:T(8,128)(2,1)S(1)}, bf16[384,1,1440]{0,2,1:T(8,128)(2,1)S(1)}, bf16[384,1,1440]{0,2,1:T(8,128)(2,1)S(1)}, bf16[384,1,1440]{0,2,1:T(8,128)(2,1)S(1)}) fusion(f32[384]{0:T(512)S(1)} %select_multiply_fusion, s32[384]{0:T(512)} %param.9), kind=kLoop, calls=%fused_computation.36 | loop fusion | flops 9953280 | bytes 4426752 | tf_op jit(solution)/shard_map/convert.2
  13.1 2.5 pad_maximum_fusion
  15.6 6.8 %copy.58 = bf16[384,2,1440]{2,1,0:T(2,128)(2,1)} copy(bf16[384,2,1440]{0,2,1:T(8,128)(2,1)} %get-tuple-element.20) | data formatting | bytes 4423680 | tf_op jit(solution)/shard_map/stack | solution.py:38
  22.4 0.0 copy-start.3
  22.4 6.0 %convert_element_type.92 = bf16[768,1440]{1,0:T(8,128)(2,1)} reshape(bf16[384,2,1440]{2,1,0:T(2,128)(2,1)} %copy.58) | data formatting | bytes 4423680 | tf_op jit(solution)/shard_map/convert_element_type | solution.py:38
  28.4 0.0 copy-done.3
  28.4 0.1 select_reduce_fusion.1
  28.5 0.1 dynamic-slice_convert_fusion
  28.6 4.8 %fusion.2 = (f32[256]{0:T(256)S(1)}, f32[256]{0:T(256)S(1)}) fusion(bf16[7,1440,256]{2,1,0:T(8,128)(2,1)} %param.7, f32[7]{0:T(128)S(1)} %dynamic-slice_convert_fusion), kind=kLoop, calls=%fused_computation.8 | loop fusion | flops 12901888 | bytes 5163036 | tf_op jit(solution)/shard_map/reduce_sum | solution.py:64
  33.4 21.9 %all-reduce = (f32[256]{0:T(256)S(1)}, f32[256]{0:T(256)S(1)}) all-reduce(f32[256]{0:T(256)S(1)} %get-tuple-element.6, f32[256]{0:T(256)S(1)} %get-tuple-element.5), channel_id=1, replica_groups=mesh['group'=2,'lat'=16] {'lat'}, use_global_device_ids=true, to_apply=%region_8.9 | all-reduce | flops 512 | bytes 4096 | tf_op jit(solution)/shard_map/psum | solution.py:63
  55.4 9.3 %convert_bitcast_fusion.1 = bf16[7,768,256]{2,1,0:T(8,128)(2,1)} fusion(bf16[7,1440,256]{2,1,0:T(8,128)(2,1)} %param.7, f32[256]{0:T(256)S(1)} %get-tuple-element.16, f32[256]{0:T(256)S(1)} %get-tuple-element.15, f32[7]{0:T(128)S(1)} %dynamic-slice_convert_fusion, bf16[768,1440]{1,0:T(8,128)(2,1)} %convert_element_type.92), kind=kOutput, calls=%fused_computation.23 | convolution fusion | flops 3977895936 | bytes 10127388 | tf_op jit(solution)/shard_map/skc,qk->sqc/dot_general | solution.py:73
  64.6 6.5 %reshape.389 = bf16[7,384,2,256]{3,2,1,0:T(2,128)(2,1)} reshape(bf16[7,768,256]{2,1,0:T(8,128)(2,1)} %convert_bitcast_fusion.1) | data formatting | bytes 5505024 | tf_op jit(solution)/shard_map/reshape | solution.py:74
  71.1 5.2 %copy.60 = bf16[7,384,2,256]{3,2,0,1:T(2,128)(2,1)} copy(bf16[7,384,2,256]{3,2,1,0:T(2,128)(2,1)} %reshape.389) | data formatting | bytes 5505024 | tf_op jit(solution)/shard_map/reshape | solution.py:74
  76.3 0.0 copy-start.1
  76.3 16.8 %all-to-all-start = ((bf16[7,384,2,256]{3,2,0,1:T(2,128)(2,1)}), bf16[7,384,2,256]{3,2,0,1:T(2,128)(2,1)}, u32[]{:S(2)}, u32[]{:S(2)}) async-start(bf16[7,384,2,256]{3,2,0,1:T(2,128)(2,1)} %copy.60), calls=%async_computation | async-start | bytes 5505024 | tf_op jit(solution)/shard_map/all_to_all | solution.py:75
  93.1 0.8 dynamic_slice.7
  93.9 0.0 copy-done.1
  93.9 0.2 copy.64
  94.0 0.1 convert_reduce_fusion
  94.1 0.1 select_reduce_fusion
  94.3 0.1 fusion.31
  94.4 60.3 %all-to-all-done = bf16[7,384,2,256]{3,2,0,1:T(2,128)(2,1)} async-done(((bf16[7,384,2,256]{3,2,0,1:T(2,128)(2,1)}), bf16[7,384,2,256]{3,2,0,1:T(2,128)(2,1)}, u32[]{:S(2)}, u32[]{:S(2)}) %all-to-all-start) | async-done | bytes 2752544 | tf_op jit(solution)/shard_map/all_to_all | solution.py:75
  154.7 2.2 copy.61
  156.9 1.8 copy.62
  158.6 0.0 copy-start.4
  158.6 4.0 %gather_fusion = bf16[96,24,2,256]{3,1,2,0:T(8,128)(2,1)} fusion(bf16[112,24,2,256]{3,1,2,0:T(8,128)(2,1)} %bitcast.59, s32[1024]{0:T(1024)S(1)} %pad_clamp_fusion.1), kind=kCustom, calls=%fused_computation | custom fusion | bytes 4718976 | tf_op jit(solution)/shard_map/jit(_take)/gather | solution.py:80
  162.7 0.0 copy-done.4
  162.7 2.3 multiply_convert_fusion
  165.0 0.0 copy-done
  165.0 6.1 %fusion = bf16[24,384,2,256]{1,3,2,0:T(8,128)(2,1)} fusion(f32[384,256]{0,1:T(8,128)S(1)} %copy.64, f32[24,384]{1,0:T(8,128)S(1)} %fusion.31, bf16[96,24,2,256]{3,1,2,0:T(8,128)(2,1)S(1)} %multiply_convert_fusion, bf16[24,96,384]{2,1,0:T(8,128)(2,1)S(1)} %copy-done), kind=kOutput, calls=%fused_computation.4 | convolution fusion | flops 920125440 | bytes 13996032 | tf_op jit(solution)/shard_map/rgl,grtc->rltc/dot_general | solution.py:84
  171.1 23.6 %copy.65 = bf16[24,384,2,256]{3,2,1,0:T(2,128)(2,1)} copy(bf16[24,384,2,256]{1,3,2,0:T(8,128)(2,1)} %fusion) | data formatting | bytes 18874368 | tf_op jit(solution)/shard_map/convert_element_type | solution.py:89
  194.7 0.0 copy-start.2
  194.7 14.6 %reshape.390 = bf16[18432,256]{1,0:T(8,128)(2,1)} reshape(bf16[24,384,2,256]{3,2,1,0:T(2,128)(2,1)} %copy.65) | data formatting | bytes 18874368 | tf_op jit(solution)/shard_map/reshape | solution.py:90
  209.3 0.0 copy-done.2
  209.3 9.9 %convolution_convert_fusion = bf16[18432,256]{1,0:T(8,128)(2,1)} fusion(bf16[18432,256]{1,0:T(8,128)(2,1)} %reshape.390, bf16[256,256]{1,0:T(8,128)(2,1)S(1)} %copy-done.2), kind=kOutput, calls=%fused_computation.2 | convolution fusion | flops 2420637696 | bytes 19005440 | tf_op jit(solution)/shard_map/dot_general | solution.py:90
  219.2 14.6 %reshape.391 = bf16[24,384,2,256]{3,2,1,0:T(2,128)(2,1)} reshape(bf16[18432,256]{1,0:T(8,128)(2,1)} %convolution_convert_fusion) | data formatting | bytes 18874368 | tf_op jit(solution)/shard_map/reshape | solution.py:91
  233.8 5.6 %convert_bitcast_fusion.2 = bf16[96,24,2,256]{3,0,2,1:T(8,128)(2,1)S(1)} fusion(bf16[24,384,2,256]{3,2,1,0:T(2,128)(2,1)} %reshape.391, bf16[24,96,384]{2,1,0:T(8,128)(2,1)S(1)} %copy-done), kind=kOutput, calls=%fused_computation.27 | convolution fusion | flops 907149312 | bytes 13565952 | tf_op jit(solution)/shard_map/rgl,rltc->grtc/dot_general | solution.py:92
  239.4 2.7 copy.67
  242.2 4.0 %gather_fusion.1 = bf16[112,24,2,256]{3,1,2,0:T(8,128)(2,1)} fusion(bf16[96,24,2,256]{3,1,2,0:T(8,128)(2,1)} %copy.67, s32[1024]{0:T(1024)S(1)} %pad_clamp_fusion), kind=kCustom, calls=%fused_computation.1 | custom fusion | bytes 5505472 | tf_op jit(solution)/shard_map/jit(_take)/gather | solution.py:97
  246.2 3.2 select_select_fusion
  249.4 4.8 %all-to-all-start.1 = ((bf16[112,24,2,256]{3,1,2,0:T(8,128)(2,1)}), bf16[112,24,2,256]{3,1,2,0:T(8,128)(2,1)}, u32[]{:S(2)}, u32[]{:S(2)}) async-start(bf16[112,24,2,256]{3,1,2,0:T(8,128)(2,1)} %select_select_fusion), calls=%async_computation.1 | async-start | bytes 5505024 | tf_op jit(solution)/shard_map/all_to_all | solution.py:101
  254.2 6.9 %copy.56 = bf16[384,2,1440]{2,1,0:T(2,128)(2,1)} copy(bf16[384,2,1440]{0,2,1:T(8,128)(2,1)} %get-tuple-element.19) | data formatting | bytes 4423680 | tf_op jit(solution)/shard_map/stack | solution.py:47
  261.1 6.0 %convert_element_type.90 = bf16[768,1440]{1,0:T(8,128)(2,1)} reshape(bf16[384,2,1440]{2,1,0:T(2,128)(2,1)} %copy.56) | data formatting | bytes 4423680 | tf_op jit(solution)/shard_map/convert_element_type | solution.py:47
  267.1 48.7 %all-to-all-done.1 = bf16[112,24,2,256]{3,1,2,0:T(8,128)(2,1)} async-done(((bf16[112,24,2,256]{3,1,2,0:T(8,128)(2,1)}), bf16[112,24,2,256]{3,1,2,0:T(8,128)(2,1)}, u32[]{:S(2)}, u32[]{:S(2)}) %all-to-all-start.1) | async-done | bytes 2752544 | tf_op jit(solution)/shard_map/all_to_all | solution.py:101
  315.7 5.8 %copy.68 = bf16[7,16,24,2,256]{4,3,2,1,0:T(2,128)(2,1)} copy(bf16[7,16,24,2,256]{4,2,3,0,1:T(8,128)(2,1)} %bitcast.18) | data formatting | bytes 5505024 | tf_op jit(solution)/shard_map/all_to_all | solution.py:101
  321.5 6.8 %reshape.392 = bf16[7,768,256]{2,1,0:T(8,128)(2,1)} reshape(bf16[7,16,24,2,256]{4,3,2,1,0:T(2,128)(2,1)} %copy.68) | data formatting | bytes 5505024 | tf_op jit(solution)/shard_map/reshape | solution.py:102
  328.3 9.1 %convert_bitcast_fusion = bf16[7,1440,256]{2,1,0:T(8,128)(2,1)} fusion(bf16[7,768,256]{2,1,0:T(8,128)(2,1)} %reshape.392, bf16[768,1440]{1,0:T(8,128)(2,1)} %convert_element_type.90), kind=kOutput, calls=%fused_computation.16 | convolution fusion | flops 3966197760 | bytes 10125312 | tf_op jit(solution)/shard_map/sqc,qk->skc/dot_general | solution.py:103
  (10 shorter events, 0.1 us)
Async XLA Ops:
  0.0 165.0 %copy-start = (bf16[24,96,384]{2,1,0:T(8,128)(2,1)S(1)}, bf16[24,96,384]{2,1,0:T(8,128)(2,1)}, u32[]{:S(2)}) copy-start(bf16[24,96,384]{2,1,0:T(8,128)(2,1)} %param.10) | copy-start | bytes 5308420
  22.4 6.0 %copy-start.3 = (s32[16]{0:T(128)S(1)}, s32[16]{0:T(128)}, u32[]{:S(2)}) copy-start(s32[16]{0:T(128)} %param.8) | copy-start | bytes 196
  76.3 17.5 %copy-start.1 = (f32[384,256]{1,0:T(8,128)S(1)}, f32[384,256]{1,0:T(8,128)}, u32[]{:S(2)}) copy-start(f32[384,256]{1,0:T(8,128)} %param.12) | copy-start | bytes 1179652
  76.3 78.3 %all-to-all-start = ((bf16[7,384,2,256]{3,2,0,1:T(2,128)(2,1)}), bf16[7,384,2,256]{3,2,0,1:T(2,128)(2,1)}, u32[]{:S(2)}, u32[]{:S(2)}) async-start(bf16[7,384,2,256]{3,2,0,1:T(2,128)(2,1)} %copy.60), calls=%async_computation | async-start | bytes 5505024 | tf_op jit(solution)/shard_map/all_to_all | solution.py:75
  158.6 4.0 %copy-start.4 = (f32[96]{0:T(128)S(1)}, f32[96]{0:T(128)}, u32[]{:S(2)}) copy-start(f32[96]{0:T(128)} %param.11) | copy-start | bytes 1156
  194.7 14.6 %copy-start.2 = (bf16[256,256]{1,0:T(8,128)(2,1)S(1)}, bf16[256,256]{1,0:T(8,128)(2,1)}, u32[]{:S(2)}) copy-start(bf16[256,256]{1,0:T(8,128)(2,1)} %param.13) | copy-start | bytes 393220
  249.4 66.3 %all-to-all-start.1 = ((bf16[112,24,2,256]{3,1,2,0:T(8,128)(2,1)}), bf16[112,24,2,256]{3,1,2,0:T(8,128)(2,1)}, u32[]{:S(2)}, u32[]{:S(2)}) async-start(bf16[112,24,2,256]{3,1,2,0:T(8,128)(2,1)} %select_select_fusion), calls=%async_computation.1 | async-start | bytes 5505024 | tf_op jit(solution)/shard_map/all_to_all | solution.py:101
where the time goes:
time: 340 us; the launch traced here: 337 us
  local copies, waits for them, and re-layouts  119 us (35%)
  waiting for transfers between devices  109 us (32%)
  matrix products  39.9 us (12%)
  other arithmetic  25.5 us (8%)
  blocking collectives  21.9 us (6%)
  starting transfers between devices  21.5 us (6%)
    all_to_all x1, waiting for transfers between devices, body(): lax.all_to_all(spectra, 'lat', split_axis=1, concat_axis=0, tiled=True)  60.3 us
    all_to_all x1, waiting for transfers between devices, body(): lax.all_to_all(outgoing, 'lat', split_axis=0, concat_axis=1, tiled=True)  48.7 us
    convert_element_type x1, local copies, waits for them, and re-layouts, body(): filtered = (coefficient * degree_mask[:, :, None, None] * spectral_gain[N...  23.6 us
    psum x1, blocking collectives, body(): lax.psum((jnp.sum(widened, axis=(0, 1)), jnp.sum(widened * widened, axis=...  21.9 us
    all_to_all x1, starting transfers between devices, body(): lax.all_to_all(spectra, 'lat', split_axis=1, concat_axis=0, tiled=True)  16.8 us
    reshape x1, local copies, waits for them, and re-layouts, body(): filtered.reshape(-1, channels)  14.6 us
    reshape x1, local copies, waits for them, and re-layouts, body(): mixed = mixed.astype(jnp.bfloat16).reshape(wave_share, degrees, 2, channels)  14.6 us
    reshape x2, local copies, waits for them, and re-layouts, body(): spectra.astype(jnp.bfloat16)  11.7 us
  transfers between devices with their start and end apart: 2, of which 2 were waited for; matrix products, arithmetic and copies ran while one was open for 4% of the time, Pallas kernels for 0%

commit v1 on v0

--- a/solution.py
+++ b/solution.py
@@ -72,7 +72,16 @@
     forward_flat = forward_table(owner_wavenumber, longitudes).reshape(2 * wave_count, longitudes)
     spectra = jnp.einsum("skc,qk->sqc", normed, forward_flat, preferred_element_type=jnp.float32)
     spectra = spectra.astype(jnp.bfloat16).reshape(slot_count, wave_count, 2, normed.shape[2])
-    received = lax.all_to_all(spectra, "lat", split_axis=1, concat_axis=0, tiled=True)
+
+    def stocks_report(piece_in, which_axis):
+        return jnp.concatenate(
+            lax.all_to_all(
+                jnp.stack(jnp.split(piece_in, lax.axis_size(which_axis), axis=1)), which_axis, 0, 0
+            ),
+            axis=0,
+        )
+
+    received = stocks_report(spectra, "lat")
     own_waves = lax.dynamic_slice_in_dim(owner_wavenumber, my_index * wave_share, wave_share)
     degree_mask = (jnp.arange(degrees, dtype=jnp.int32)[None, :] >= own_waves[:, None]).astype(
         jnp.float32

time: 340 us -> 362 us (1.065)
  local copies, waits for them, and re-layouts: 119 us -> 141 us
    unnamed x11 -> x26, local copies, waits for them, and re-layouts: 0.18 us -> 25.8 us
    reshape x2 -> x1, local copies, waits for them, and re-layouts: 11.7 us -> 6.53 us  [body(): spectra.astype(jnp.bfloat16)]
where the time goes in v1:
time: 362 us; the launch traced here: 359 us
  local copies, waits for them, and re-layouts  141 us (39%)
  waiting for transfers between devices  109 us (30%)
  matrix products  39.9 us (11%)
  other arithmetic  25.5 us (7%)
  blocking collectives  21.9 us (6%)
  starting transfers between devices  21.5 us (6%)
    all_to_all x1, waiting for transfers between devices, stocks_report(): lax.all_to_all(jnp.stack(jnp.split(piece_in, lax.axis_size(which_axis), a...  60.3 us
    all_to_all x1, waiting for transfers between devices, body(): lax.all_to_all(outgoing, 'lat', split_axis=0, concat_axis=1, tiled=True)  48.7 us
    unnamed x26, local copies, waits for them, and re-layouts  25.8 us
    convert_element_type x1, local copies, waits for them, and re-layouts, body(): filtered = (coefficient * degree_mask[:, :, None, None] * spectral_gain[N...  23.6 us
    psum x1, blocking collectives, body(): lax.psum((jnp.sum(widened, axis=(0, 1)), jnp.sum(widened * widened, axis=...  21.9 us
    all_to_all x1, starting transfers between devices, stocks_report(): lax.all_to_all(jnp.stack(jnp.split(piece_in, lax.axis_size(which_axis), a...  16.8 us
    reshape x1, local copies, waits for them, and re-layouts, body(): filtered.reshape(-1, channels)  14.6 us
    reshape x1, local copies, waits for them, and re-layouts, body(): mixed = mixed.astype(jnp.bfloat16).reshape(wave_share, degrees, 2, channels)  14.6 us
  transfers between devices with their start and end apart: 2, of which 2 were waited for; matrix products, arithmetic and copies ran while one was open for 4% of the time, Pallas kernels for 0%

profile of v1, /device:TPU:15, one launch (start us, length us, event | category | flops | bytes accessed | tf_op | source)
XLA Modules:
  0.0 359.3 jit_solution(7982414762533243867)
XLA Ops:
  0.0 0.0 copy-start
  0.0 0.9 copy.33
  0.9 0.1 reduce
  1.0 0.7 sub.72
  1.7 0.7 select_multiply_fusion
  2.4 10.7 %multiply_convert_fusion.4 = (bf16[384,1,1440]{0,2,1:T(8,128)(2,1)S(1)}, bf16[384,1,1440]{0,2,1:T(8,128)(2,1)S(1)}, bf16[384,1,1440]{0,2,1:T(8,128)(2,1)S(1)}, bf16[384,1,1440]{0,2,1:T(8,128)(2,1)S(1)}) fusion(f32[384]{0:T(512)S(1)} %select_multiply_fusion, s32[384]{0:T(512)} %param.9), kind=kLoop, calls=%fused_computation.36 | loop fusion | flops 9953280 | bytes 4426752 | tf_op jit(solution)/shard_map/convert.2
  13.1 2.5 pad_maximum_fusion
  15.6 6.8 %copy.34 = bf16[384,2,1440]{2,1,0:T(2,128)(2,1)} copy(bf16[384,2,1440]{0,2,1:T(8,128)(2,1)} %get-tuple-element.20) | data formatting | bytes 4423680 | tf_op jit(solution)/shard_map/stack | solution.py:38
  22.4 0.0 copy-start.3
  22.4 6.0 %convert_element_type.92 = bf16[768,1440]{1,0:T(8,128)(2,1)} reshape(bf16[384,2,1440]{2,1,0:T(2,128)(2,1)} %copy.34) | data formatting | bytes 4423680 | tf_op jit(solution)/shard_map/convert_element_type | solution.py:38
  28.4 0.0 copy-done.3
  28.4 0.1 select_reduce_fusion.1
  28.5 0.1 dynamic-slice_convert_fusion
  28.6 4.8 %fusion.2 = (f32[256]{0:T(256)S(1)}, f32[256]{0:T(256)S(1)}) fusion(bf16[7,1440,256]{2,1,0:T(8,128)(2,1)} %param.7, f32[7]{0:T(128)S(1)} %dynamic-slice_convert_fusion), kind=kLoop, calls=%fused_computation.8 | loop fusion | flops 12901888 | bytes 5163036 | tf_op jit(solution)/shard_map/reduce_sum | solution.py:64
  33.4 21.9 %all-reduce = (f32[256]{0:T(256)S(1)}, f32[256]{0:T(256)S(1)}) all-reduce(f32[256]{0:T(256)S(1)} %get-tuple-element.6, f32[256]{0:T(256)S(1)} %get-tuple-element.5), channel_id=1, replica_groups=mesh['group'=2,'lat'=16] {'lat'}, use_global_device_ids=true, to_apply=%region_8.9 | all-reduce | flops 512 | bytes 4096 | tf_op jit(solution)/shard_map/psum | solution.py:63
  55.4 9.3 %convert_bitcast_fusion.1 = bf16[7,768,256]{2,1,0:T(8,128)(2,1)} fusion(bf16[7,1440,256]{2,1,0:T(8,128)(2,1)} %param.7, f32[256]{0:T(256)S(1)} %get-tuple-element.16, f32[256]{0:T(256)S(1)} %get-tuple-element.15, f32[7]{0:T(128)S(1)} %dynamic-slice_convert_fusion, bf16[768,1440]{1,0:T(8,128)(2,1)} %convert_element_type.92), kind=kOutput, calls=%fused_computation.23 | convolution fusion | flops 3977895936 | bytes 10127388 | tf_op jit(solution)/shard_map/skc,qk->sqc/dot_general | solution.py:73
  64.6 6.5 %reshape.392 = bf16[7,384,2,256]{3,2,1,0:T(2,128)(2,1)} reshape(bf16[7,768,256]{2,1,0:T(8,128)(2,1)} %convert_bitcast_fusion.1) | data formatting | bytes 5505024 | tf_op jit(solution)/shard_map/reshape | solution.py:74
  71.1 1.7 fusion.46
  72.9 1.7 fusion.45
  74.6 1.7 fusion.44
  76.3 1.7 fusion.43
  78.0 1.7 fusion.42
  79.7 1.7 fusion.41
  81.4 1.7 fusion.40
  83.1 1.7 fusion.39
  84.8 1.7 fusion.38
  86.5 1.7 fusion.37
  88.2 1.7 fusion.36
  89.9 1.7 fusion.35
  91.6 1.7 fusion.34
  93.3 1.7 fusion.33
  95.0 1.7 fusion.32
  96.8 1.7 fusion.31
  98.5 0.0 copy-start.1
  98.5 16.8 %all-to-all-start = ((bf16[16,7,24,2,256]{4,3,2,1,0:T(2,128)(2,1)}), bf16[16,7,24,2,256]{4,3,2,1,0:T(2,128)(2,1)}, u32[]{:S(2)}, u32[]{:S(2)}) async-start(bf16[16,7,24,2,256]{4,3,2,1,0:T(2,128)(2,1)} %fusion.31), calls=%async_computation | async-start | bytes 5505024 | tf_op jit(solution)/shard_map/all_to_all | solution.py:78
  115.2 0.8 dynamic_slice.7
  116.0 0.0 copy-done.1
  116.0 0.2 copy.38
  116.1 0.1 convert_reduce_fusion
  116.2 0.1 select_reduce_fusion
  116.4 0.1 fusion.47
  116.5 60.3 %all-to-all-done = bf16[16,7,24,2,256]{4,3,2,1,0:T(2,128)(2,1)} async-done(((bf16[16,7,24,2,256]{4,3,2,1,0:T(2,128)(2,1)}), bf16[16,7,24,2,256]{4,3,2,1,0:T(2,128)(2,1)}, u32[]{:S(2)}, u32[]{:S(2)}) %all-to-all-start) | async-done | bytes 2752544 | tf_op jit(solution)/shard_map/all_to_all | solution.py:78
  176.8 3.8 %copy.36 = bf16[16,7,24,2,256]{4,2,3,1,0:T(8,128)(2,1)} copy(bf16[16,7,24,2,256]{4,3,2,1,0:T(2,128)(2,1)} %all-to-all-done) | data formatting | bytes 5505024 | tf_op jit(solution)/shard_map/all_to_all | solution.py:78
  180.6 4.0 %gather_fusion = bf16[96,24,2,256]{3,1,2,0:T(8,128)(2,1)} fusion(bf16[112,24,2,256]{3,1,2,0:T(8,128)(2,1)} %bitcast.119, s32[1024]{0:T(1024)S(1)} %pad_clamp_fusion.1), kind=kCustom, calls=%fused_computation | custom fusion | bytes 4718976 | tf_op jit(solution)/shard_map/jit(_take)/gather | solution.py:89
  184.6 0.0 copy-done.4
  184.6 2.3 multiply_convert_fusion
  186.9 0.0 copy-done
  186.9 6.1 %fusion = bf16[24,384,2,256]{1,3,2,0:T(8,128)(2,1)} fusion(f32[384,256]{0,1:T(8,128)S(1)} %copy.38, f32[24,384]{1,0:T(8,128)S(1)} %fusion.47, bf16[96,24,2,256]{3,1,2,0:T(8,128)(2,1)S(1)} %multiply_convert_fusion, bf16[24,96,384]{2,1,0:T(8,128)(2,1)S(1)} %copy-done), kind=kOutput, calls=%fused_computation.4 | convolution fusion | flops 920125440 | bytes 13996032 | tf_op jit(solution)/shard_map/rgl,grtc->rltc/dot_general | solution.py:93
  193.0 23.6 %copy.39 = bf16[24,384,2,256]{3,2,1,0:T(2,128)(2,1)} copy(bf16[24,384,2,256]{1,3,2,0:T(8,128)(2,1)} %fusion) | data formatting | bytes 18874368 | tf_op jit(solution)/shard_map/convert_element_type | solution.py:98
  216.6 14.6 %reshape.394 = bf16[18432,256]{1,0:T(8,128)(2,1)} reshape(bf16[24,384,2,256]{3,2,1,0:T(2,128)(2,1)} %copy.39) | data formatting | bytes 18874368 | tf_op jit(solution)/shard_map/reshape | solution.py:99
  231.2 0.0 copy-done.2
  231.2 9.9 %convolution_convert_fusion = bf16[18432,256]{1,0:T(8,128)(2,1)} fusion(bf16[18432,256]{1,0:T(8,128)(2,1)} %reshape.394, bf16[256,256]{1,0:T(8,128)(2,1)S(1)} %copy-done.2), kind=kOutput, calls=%fused_computation.2 | convolution fusion | flops 2420637696 | bytes 19005440 | tf_op jit(solution)/shard_map/dot_general | solution.py:99
  241.2 14.6 %reshape.395 = bf16[24,384,2,256]{3,2,1,0:T(2,128)(2,1)} reshape(bf16[18432,256]{1,0:T(8,128)(2,1)} %convolution_convert_fusion) | data formatting | bytes 18874368 | tf_op jit(solution)/shard_map/reshape | solution.py:100
  255.8 5.6 %convert_bitcast_fusion.2 = bf16[96,24,2,256]{3,0,2,1:T(8,128)(2,1)S(1)} fusion(bf16[24,384,2,256]{3,2,1,0:T(2,128)(2,1)} %reshape.395, bf16[24,96,384]{2,1,0:T(8,128)(2,1)S(1)} %copy-done), kind=kOutput, calls=%fused_computation.27 | convolution fusion | flops 907149312 | bytes 13565952 | tf_op jit(solution)/shard_map/rgl,rltc->grtc/dot_general | solution.py:101
  261.3 2.7 copy.41
  264.1 4.0 %gather_fusion.1 = bf16[112,24,2,256]{3,1,2,0:T(8,128)(2,1)} fusion(bf16[96,24,2,256]{3,1,2,0:T(8,128)(2,1)} %copy.41, s32[1024]{0:T(1024)S(1)} %pad_clamp_fusion), kind=kCustom, calls=%fused_computation.1 | custom fusion | bytes 5505472 | tf_op jit(solution)/shard_map/jit(_take)/gather | solution.py:106
  268.1 3.2 select_select_fusion
  271.3 4.8 %all-to-all-start.1 = ((bf16[112,24,2,256]{3,1,2,0:T(8,128)(2,1)}), bf16[112,24,2,256]{3,1,2,0:T(8,128)(2,1)}, u32[]{:S(2)}, u32[]{:S(2)}) async-start(bf16[112,24,2,256]{3,1,2,0:T(8,128)(2,1)} %select_select_fusion), calls=%async_computation.1 | async-start | bytes 5505024 | tf_op jit(solution)/shard_map/all_to_all | solution.py:110
  276.1 6.9 %copy.32 = bf16[384,2,1440]{2,1,0:T(2,128)(2,1)} copy(bf16[384,2,1440]{0,2,1:T(8,128)(2,1)} %get-tuple-element.19) | data formatting | bytes 4423680 | tf_op jit(solution)/shard_map/stack | solution.py:47
  283.0 6.0 %convert_element_type.90 = bf16[768,1440]{1,0:T(8,128)(2,1)} reshape(bf16[384,2,1440]{2,1,0:T(2,128)(2,1)} %copy.32) | data formatting | bytes 4423680 | tf_op jit(solution)/shard_map/convert_element_type | solution.py:47
  289.0 48.7 %all-to-all-done.1 = bf16[112,24,2,256]{3,1,2,0:T(8,128)(2,1)} async-done(((bf16[112,24,2,256]{3,1,2,0:T(8,128)(2,1)}), bf16[112,24,2,256]{3,1,2,0:T(8,128)(2,1)}, u32[]{:S(2)}, u32[]{:S(2)}) %all-to-all-start.1) | async-done | bytes 2752544 | tf_op jit(solution)/shard_map/all_to_all | solution.py:110
  337.7 5.8 %copy.42 = bf16[7,16,24,2,256]{4,3,2,1,0:T(2,128)(2,1)} copy(bf16[7,16,24,2,256]{4,2,3,0,1:T(8,128)(2,1)} %bitcast.32) | data formatting | bytes 5505024 | tf_op jit(solution)/shard_map/all_to_all | solution.py:110
  343.4 6.8 %reshape.396 = bf16[7,768,256]{2,1,0:T(8,128)(2,1)} reshape(bf16[7,16,24,2,256]{4,3,2,1,0:T(2,128)(2,1)} %copy.42) | data formatting | bytes 5505024 | tf_op jit(solution)/shard_map/reshape | solution.py:111
  350.2 9.1 %convert_bitcast_fusion = bf16[7,1440,256]{2,1,0:T(8,128)(2,1)} fusion(bf16[7,768,256]{2,1,0:T(8,128)(2,1)} %reshape.396, bf16[768,1440]{1,0:T(8,128)(2,1)} %convert_element_type.90), kind=kOutput, calls=%fused_computation.16 | convolution fusion | flops 3966197760 | bytes 10125312 | tf_op jit(solution)/shard_map/sqc,qk->skc/dot_general | solution.py:112
  (12 shorter events, 0.1 us)
Async XLA Ops:
  0.0 186.9 %copy-start = (bf16[24,96,384]{2,1,0:T(8,128)(2,1)S(1)}, bf16[24,96,384]{2,1,0:T(8,128)(2,1)}, u32[]{:S(2)}) copy-start(bf16[24,96,384]{2,1,0:T(8,128)(2,1)} %param.10) | copy-start | bytes 5308420
  22.4 6.0 %copy-start.3 = (s32[16]{0:T(128)S(1)}, s32[16]{0:T(128)}, u32[]{:S(2)}) copy-start(s32[16]{0:T(128)} %param.8) | copy-start | bytes 196
  98.5 17.5 %copy-start.1 = (f32[384,256]{1,0:T(8,128)S(1)}, f32[384,256]{1,0:T(8,128)}, u32[]{:S(2)}) copy-start(f32[384,256]{1,0:T(8,128)} %param.12) | copy-start | bytes 1179652
  98.5 78.3 %all-to-all-start = ((bf16[16,7,24,2,256]{4,3,2,1,0:T(2,128)(2,1)}), bf16[16,7,24,2,256]{4,3,2,1,0:T(2,128)(2,1)}, u32[]{:S(2)}, u32[]{:S(2)}) async-start(bf16[16,7,24,2,256]{4,3,2,1,0:T(2,128)(2,1)} %fusion.31), calls=%async_computation | async-start | bytes 5505024 | tf_op jit(solution)/shard_map/all_to_all | solution.py:78
  180.6 4.0 %copy-start.4 = (f32[96]{0:T(128)S(1)}, f32[96]{0:T(128)}, u32[]{:S(2)}) copy-start(f32[96]{0:T(128)} %param.11) | copy-start | bytes 1156
  216.6 14.6 %copy-start.2 = (bf16[256,256]{1,0:T(8,128)(2,1)S(1)}, bf16[256,256]{1,0:T(8,128)(2,1)}, u32[]{:S(2)}) copy-start(bf16[256,256]{1,0:T(8,128)(2,1)} %param.13) | copy-start | bytes 393220
  271.3 66.3 %all-to-all-start.1 = ((bf16[112,24,2,256]{3,1,2,0:T(8,128)(2,1)}), bf16[112,24,2,256]{3,1,2,0:T(8,128)(2,1)}, u32[]{:S(2)}, u32[]{:S(2)}) async-start(bf16[112,24,2,256]{3,1,2,0:T(8,128)(2,1)} %select_select_fusion), calls=%async_computation.1 | async-start | bytes 5505024 | tf_op jit(solution)/shard_map/all_to_all | solution.py:110
